TPU v7x, 32 devices: a whole 2x2x4 slice. The times are simulated.
32 devices in a mesh: rep: 4 (over x, core), fsdp: 8 (over z, y).
Axes of the slice: x: 2, y: 2, z: 4, core: 2. Of those that a mesh axis runs over, the one named last changes fastest.
Arguments:
- features: bfloat16 [4096, 1280], P(('rep', 'fsdp')), may hold values from -6 to 6
- cotangent: bfloat16 [4096, 1280], P(('rep', 'fsdp')), may hold values from -1 to 1
- clip_lengths: int32 [4, 8], P('rep'), may hold values from 96 to 128, as said below
- group_clips: int32 [4], P('rep'), may hold values from 6 to 8, as said below
- outer_attention: float32 [2, 1280, 5120], P(None, 'fsdp')
- outer_feedforward: float32 [2, 1280, 10240], P(None, 'fsdp')
- outer_vectors: float32 [2, 12, 1280], P(None, None, 'fsdp')
- moments_attention: float32 [4, 2, 1280, 5120], P('rep', None, 'fsdp')
- moments_feedforward: float32 [4, 2, 1280, 10240], P('rep', None, 'fsdp')
- moments_vectors: float32 [4, 2, 12, 1280], P('rep', None, None, 'fsdp')
Outputs:
- block_output: bfloat16 [4096, 1280], P(('rep', 'fsdp'))
- input_grad: float32 [4096, 1280], P(('rep', 'fsdp'))
- group_attention: float32 [4, 3, 1280, 5120], P('rep', None, 'fsdp')
- group_feedforward: float32 [4, 3, 1280, 10240], P('rep', None, 'fsdp')
- group_vectors: float32 [4, 3, 12, 1280], P('rep', None, None, 'fsdp')
- group_weights: float32 [4, 1280, 15372], P('rep', 'fsdp')
- next_attention: float32 [3, 1280, 5120], P(None, 'fsdp')
- next_feedforward: float32 [3, 1280, 10240], P(None, 'fsdp')
- next_vectors: float32 [3, 12, 1280], P(None, None, 'fsdp')
- copy_attention: bfloat16 [1280, 5120], P('fsdp')
- copy_feedforward: bfloat16 [1280, 10240], P('fsdp')
- copy_vectors: bfloat16 [12, 1280], P(None, 'fsdp')
Inputs may be any that keep to these rules, and one draw needn't show every extreme that they name: `clip_lengths`: some clip has exactly 128 valid tokens and some exactly 96. Group g holds clips in its slots 0 to group_clips[g] - 1 and none in the others; some group has all 8 and some 8 - 2.
All inputs are finite; a program needn't handle non-finite values.
Results may differ from a plain program's by a relative error of at most 0.012.
The roundings to bfloat16 on the way count: a program that leaves them out, or rounds other values in their place, can miss the bound.
Values may be sent and summed in bfloat16 or wider, within the bound.
A program may use at most 448 MiB of HBM per device.

v0:
```python
from functools import partial
import jax
import jax.numpy as jnp
from jax import lax
from jax.sharding import PartitionSpec as P

D = 1280
HEADS = 16
HD = 80
FF = 5120
STEP = 3
NORM_EPS = 1e-05
MASKED = -1e30
ADAM_RATE = 0.03
ADAM_DECAY = 0.1
ADAM_BETA = 0.5
ADAM_EPS = 1e-08
OUTER_RATE = 0.7
OUTER_MOMENTUM = 0.5


def contract_last(left, right):
    return lax.dot_general(
        left, right, (((1,), (1,)), ((), ())), preferred_element_type=jnp.float32
    )


def contract_rows(left, right):
    return lax.dot_general(
        left, right, (((0,), (0,)), ((), ())), preferred_element_type=jnp.float32
    )


def normalize(inputs, gain_row, shift_row):
    average = jnp.mean(inputs, axis=-1, keepdims=True)
    centered = inputs - average
    reciprocal = lax.rsqrt(jnp.mean(centered * centered, axis=-1, keepdims=True) + NORM_EPS)
    unit_rows = centered * reciprocal
    return (unit_rows * gain_row + shift_row, unit_rows, reciprocal)


def normalize_back(incoming, unit_rows, reciprocal, gain_row):
    scaled = incoming * gain_row
    centered = scaled - jnp.mean(scaled, axis=-1, keepdims=True)
    return reciprocal * (
        centered - unit_rows * jnp.mean(scaled * unit_rows, axis=-1, keepdims=True)
    )


def adamw_step(weight, gradient, moments, decay_rate):
    first_moment = ADAM_BETA * moments[0] + (1.0 - ADAM_BETA) * gradient
    second_moment = ADAM_BETA * moments[1] + (1.0 - ADAM_BETA) * gradient * gradient
    correction = 1.0 - ADAM_BETA**STEP
    direction = first_moment / correction / (jnp.sqrt(second_moment / correction) + ADAM_EPS)
    return (weight - ADAM_RATE * (direction + decay_rate * weight), first_moment, second_moment)


def outer_step(master, mean_delta, momentum_old):
    momentum = OUTER_MOMENTUM * momentum_old - mean_delta
    outer_next = master - OUTER_RATE * (OUTER_MOMENTUM * momentum - mean_delta)
    return jnp.stack([mean_delta, momentum, outer_next])


def shards(
    features,
    cotangent,
    clip_lengths,
    group_clips,
    outer_attention,
    outer_feedforward,
    outer_vectors,
    moments_attention,
    moments_feedforward,
    moments_vectors,
):
    tokens_here = features.shape[0]
    scale = HD ** (-0.5)
    clip_slot = lax.axis_index("fsdp")
    clip_length = lax.dynamic_index_in_dim(clip_lengths[0], clip_slot, keepdims=False)
    live_clip = clip_slot < group_clips[0]
    positions = jnp.arange(tokens_here, dtype=jnp.int32)
    key_valid = positions < clip_length
    row_valid = key_valid & live_clip
    masters = (outer_attention[0], outer_feedforward[0], outer_vectors[0])
    copies = (
        masters[0].astype(jnp.bfloat16),
        masters[1].astype(jnp.bfloat16),
        masters[2].astype(jnp.bfloat16),
    )
    full_attention, full_feedforward, full_vectors = (
        lax.all_gather(copies[0], "fsdp", axis=0, tiled=True),
        lax.all_gather(copies[1], "fsdp", axis=0, tiled=True),
        lax.all_gather(copies[2], "fsdp", axis=1, tiled=True),
    )
    vectors = full_vectors.astype(jnp.float32)
    inputs = features.astype(jnp.float32)
    normed_one, unit_one, scale_one = normalize(inputs, vectors[0], vectors[1])
    layer_one = normed_one.astype(jnp.bfloat16)
    qkv_bias = jnp.concatenate([vectors[2], jnp.zeros_like(vectors[2]), vectors[3]])
    projected = (
        jnp.dot(layer_one, full_attention[:, : 3 * D], preferred_element_type=jnp.float32)
        + qkv_bias
    ).astype(jnp.bfloat16)
    query_heads = projected[:, :D].reshape(tokens_here, HEADS, HD)
    key_heads = projected[:, D : 2 * D].reshape(tokens_here, HEADS, HD)
    value_heads = projected[:, 2 * D :].reshape(tokens_here, HEADS, HD)

    def score_block():
        raw_scores = (
            jnp.einsum("qhd,khd->hqk", query_heads, key_heads, preferred_element_type=jnp.float32)
            * scale
        )
        return jnp.where(key_valid[None, None, :], raw_scores, MASKED)

    scores = score_block()
    top_score = jnp.max(scores, axis=-1, keepdims=True)
    exponent = jnp.exp(scores - top_score)
    totals = jnp.sum(exponent, axis=-1, keepdims=True)
    attention_probs = exponent / totals
    log_totals = top_score + jnp.log(totals)
    attended = jnp.einsum(
        "hqk,khd->qhd",
        attention_probs.astype(jnp.bfloat16),
        value_heads,
        preferred_element_type=jnp.float32,
    )
    attended = attended.reshape(tokens_here, D).astype(jnp.bfloat16)
    attention_branch = contract_last(attended, full_attention[:, 3 * D :]) + vectors[4]
    middle = inputs + attention_branch
    normed_two, unit_two, scale_two = normalize(middle, vectors[5], vectors[6])
    layer_two = normed_two.astype(jnp.bfloat16)
    pre_activation = jnp.dot(
        layer_two, full_feedforward[:, :FF], preferred_element_type=jnp.float32
    ) + vectors[8:].reshape(FF)
    activation, gelu_backward = jax.vjp(partial(jax.nn.gelu, approximate=False), pre_activation)
    activation_low = activation.astype(jnp.bfloat16)
    feedforward_branch = contract_last(activation_low, full_feedforward[:, FF:]) + vectors[7]
    block_output = (middle + feedforward_branch).astype(jnp.bfloat16)
    back_attention, back_feedforward, back_vectors = (
        lax.all_gather(copies[0], "fsdp", axis=0, tiled=True),
        lax.all_gather(copies[1], "fsdp", axis=0, tiled=True),
        lax.all_gather(copies[2], "fsdp", axis=1, tiled=True),
    )
    gain_rows = back_vectors.astype(jnp.float32)
    upstream = cotangent.astype(jnp.float32) * row_valid[:, None].astype(jnp.float32)
    upstream_low = upstream.astype(jnp.bfloat16)
    grad_down_bias = jnp.sum(upstream_low, axis=0, dtype=jnp.float32)
    grad_activation = jnp.dot(
        upstream_low, back_feedforward[:, FF:], preferred_element_type=jnp.float32
    )
    grad_pre = gelu_backward(grad_activation)[0].astype(jnp.bfloat16)
    grad_up_bias = jnp.sum(grad_pre, axis=0, dtype=jnp.float32)
    grad_two = contract_last(grad_pre, back_feedforward[:, :FF])
    grad_gain_two = jnp.sum(grad_two * unit_two, axis=0)
    grad_shift_two = jnp.sum(grad_two, axis=0)
    grad_middle = upstream + normalize_back(grad_two, unit_two, scale_two, gain_rows[5])
    middle_low = grad_middle.astype(jnp.bfloat16)
    grad_out_bias = jnp.sum(middle_low, axis=0, dtype=jnp.float32)
    grad_attended = jnp.dot(
        middle_low, back_attention[:, 3 * D :], preferred_element_type=jnp.float32
    ).astype(jnp.bfloat16)
    grad_heads = grad_attended.reshape(tokens_here, HEADS, HD)
    attention_probs = jnp.exp(score_block() - log_totals)
    grad_probs = jnp.einsum(
        "qhd,khd->hqk", grad_heads, value_heads, preferred_element_type=jnp.float32
    )
    row_dot = jnp.sum(attention_probs * grad_probs, axis=-1, keepdims=True)
    grad_scores = (attention_probs * (grad_probs - row_dot)).astype(jnp.bfloat16)
    grad_queries = (
        jnp.einsum("hqk,khd->qhd", grad_scores, key_heads, preferred_element_type=jnp.float32)
        * scale
    ).reshape(tokens_here, D)
    grad_keys = (
        jnp.einsum("hqk,qhd->khd", grad_scores, query_heads, preferred_element_type=jnp.float32)
        * scale
    ).reshape(tokens_here, D)
    grad_values = jnp.einsum(
        "hqk,qhd->khd",
        attention_probs.astype(jnp.bfloat16),
        grad_heads,
        preferred_element_type=jnp.float32,
    ).reshape(tokens_here, D)
    grad_qkv = jnp.concatenate([grad_queries, grad_keys, grad_values], axis=1).astype(jnp.bfloat16)
    grad_query_bias = jnp.sum(grad_qkv[:, :D], axis=0, dtype=jnp.float32)
    grad_value_bias = jnp.sum(grad_qkv[:, 2 * D :], axis=0, dtype=jnp.float32)
    grad_one = contract_last(grad_qkv, back_attention[:, : 3 * D])
    grad_gain_one = jnp.sum(grad_one * unit_one, axis=0)
    grad_shift_one = jnp.sum(grad_one, axis=0)
    input_grad = grad_middle + normalize_back(grad_one, unit_one, scale_one, gain_rows[0])
    vector_rows = jnp.stack(
        [
            grad_gain_one,
            grad_shift_one,
            grad_query_bias,
            grad_value_bias,
            grad_out_bias,
            grad_gain_two,
            grad_shift_two,
            grad_down_bias,
        ]
    )
    grad_vectors = jnp.concatenate([vector_rows, grad_up_bias.reshape(4, D)], axis=0)
    owned_attention = lax.psum_scatter(
        jnp.concatenate(
            [contract_rows(layer_one, grad_qkv), contract_rows(middle_low, attended)], axis=1
        ),
        "fsdp",
        scatter_dimension=0,
        tiled=True,
    )
    owned_feedforward = lax.psum_scatter(
        jnp.concatenate(
            [contract_rows(layer_two, grad_pre), contract_rows(upstream_low, activation_low)],
            axis=1,
        ),
        "fsdp",
        scatter_dimension=0,
        tiled=True,
    )
    owned_vectors = lax.psum_scatter(grad_vectors, "fsdp", scatter_dimension=1, tiled=True)
    new_attention, first_attention, second_attention = adamw_step(
        masters[0], owned_attention, moments_attention[0], ADAM_DECAY
    )
    new_feedforward, first_feedforward, second_feedforward = adamw_step(
        masters[1], owned_feedforward, moments_feedforward[0], ADAM_DECAY
    )
    new_vectors, first_vectors, second_vectors = adamw_step(
        masters[2], owned_vectors, moments_vectors[0], 0.0
    )
    summed = (
        lax.psum_scatter(
            (new_attention - masters[0]).astype(jnp.bfloat16),
            "rep",
            scatter_dimension=1,
            tiled=True,
        ).astype(jnp.float32),
        lax.psum_scatter(
            (new_feedforward - masters[1]).astype(jnp.bfloat16),
            "rep",
            scatter_dimension=1,
            tiled=True,
        ).astype(jnp.float32),
        lax.psum_scatter(
            (new_vectors - masters[2]).astype(jnp.bfloat16), "rep", scatter_dimension=0, tiled=True
        ).astype(jnp.float32),
    )
    replicas = lax.axis_size("rep")
    replica_index = lax.axis_index("rep")
    attention_cols = 4 * D // replicas
    feedforward_cols = 2 * FF // replicas
    vector_count = 12 // replicas

    def owned_part(array, dim, count):
        return lax.dynamic_slice_in_dim(array, replica_index * count, count, dim)

    part_attention = outer_step(
        owned_part(masters[0], 1, attention_cols),
        summed[0] / replicas,
        owned_part(outer_attention[1], 1, attention_cols),
    )
    part_feedforward = outer_step(
        owned_part(masters[1], 1, feedforward_cols),
        summed[1] / replicas,
        owned_part(outer_feedforward[1], 1, feedforward_cols),
    )
    part_vectors = outer_step(
        owned_part(masters[2], 0, vector_count),
        summed[2] / replicas,
        owned_part(outer_vectors[1], 0, vector_count),
    )
    next_attention, next_feedforward, next_vectors = (
        lax.all_gather(part_attention, "rep", axis=2, tiled=True),
        lax.all_gather(part_feedforward, "rep", axis=2, tiled=True),
        lax.all_gather(part_vectors, "rep", axis=1, tiled=True),
    )
    copy_attention = next_attention[2].astype(jnp.bfloat16)
    copy_feedforward = next_feedforward[2].astype(jnp.bfloat16)
    copy_vectors = next_vectors[2].astype(jnp.bfloat16)
    group_attention = jnp.stack([owned_attention, first_attention, second_attention])[None]
    group_feedforward = jnp.stack([owned_feedforward, first_feedforward, second_feedforward])[None]
    group_vectors = jnp.stack([owned_vectors, first_vectors, second_vectors])[None]
    group_weights = jnp.concatenate([new_attention, new_feedforward, new_vectors.T], axis=1)[None]
    return (
        block_output,
        input_grad,
        group_attention,
        group_feedforward,
        group_vectors,
        group_weights,
        next_attention,
        next_feedforward,
        next_vectors,
        copy_attention,
        copy_feedforward,
        copy_vectors,
    )


def solution(mesh):
    in_specs = (
        P(("rep", "fsdp"), None),
        P(("rep", "fsdp"), None),
        P("rep", None),
        P("rep"),
        P(None, "fsdp", None),
        P(None, "fsdp", None),
        P(None, None, "fsdp"),
        P("rep", None, "fsdp", None),
        P("rep", None, "fsdp", None),
        P("rep", None, None, "fsdp"),
    )
    out_specs = (
        P(("rep", "fsdp"), None),
        P(("rep", "fsdp"), None),
        P("rep", None, "fsdp", None),
        P("rep", None, "fsdp", None),
        P("rep", None, None, "fsdp"),
        P("rep", "fsdp", None),
        P(None, "fsdp", None),
        P(None, "fsdp", None),
        P(None, None, "fsdp"),
        P("fsdp", None),
        P("fsdp", None),
        P(None, "fsdp"),
    )
    return jax.shard_map(shards, mesh=mesh, in_specs=in_specs, out_specs=out_specs, check_vma=False)
```

profile of v0, /device:TPU:0, one launch (start us, length us, event | category | flops | bytes accessed | tf_op | source)
XLA Modules:
  0.0 2351.6 jit_solution(7769149582330624274)
XLA Ops:
  17.1 33.6 %all-gather = bf16[8,160,12]{1,2,0:T(8,128)(2,1)S(1)} all-gather(bf16[1,160,12]{1,2,0:T(8,128)(2,1)S(1)} %copy.142), channel_id=1, replica_groups=mesh['rep'=4,'fsdp'=8] {'fsdp'}, dimensions={0}, use_global_device_ids=true | all-gather | bytes 34560 | tf_op jit(solution)/shard_map/all_gather | solution.py:93
  54.6 141.9 %all-gather.6.cloned.1.call-done = bf16[1280,5120]{1,0:T(8,128)(2,1)} async-done(((bf16[160,5120]{1,0:T(8,128)(2,1)}), bf16[1280,5120]{1,0:T(8,128)(2,1)}) %all-gather.6.cloned.1.call-update) | async-done | bytes 13107216 | tf_op jit(solution)/shard_map/all_gather | solution.py:91
  207.5 489.4 %all-gather.8.cloned.1.call-done = bf16[1280,10240]{1,0:T(8,128)(2,1)} async-done(((bf16[160,10240]{1,0:T(8,128)(2,1)}), bf16[1280,10240]{1,0:T(8,128)(2,1)}) %all-gather.8.cloned.1.call-update) | async-done | bytes 26214416 | tf_op jit(solution)/shard_map/all_gather | solution.py:92
  702.8 11.3 convert_reduce_fusion
  714.1 8.4 multiply_reduce_fusion.1
  736.2 9.2 pad_maximum_fusion.1
  745.6 13.1 fusion.115
  758.6 12.3 fusion.110
  770.9 34.1 %pad_maximum_fusion = f32[1280,10240]{1,0:T(8,128)} fusion(f32[1280,5120]{1,0:T(8,128)} %fusion.110, f32[1280,5120]{1,0:T(8,128)} %fusion.115), kind=kLoop, calls=%fused_computation | loop fusion | flops 13107200 | bytes 104857600 | tf_op jit(solution)/shard_map/concatenate | solution.py:212
  805.1 358.9 %reduce-scatter.7.cloned.1.call-done = f32[160,5120]{1,0:T(8,128)} async-done(((f32[1280,5120]{1,0:T(8,128)}), f32[160,5120]{1,0:T(8,128)}) %reduce-scatter.7.cloned.1.call-update) | async-done | bytes 3276816 | tf_op jit(solution)/shard_map/reduce_scatter | solution.py:203
  1164.0 9.6 fusion.29
  1173.7 811.0 %reduce-scatter.9.cloned.1.call-done = f32[160,10240]{1,0:T(8,128)} async-done(((f32[1280,10240]{1,0:T(8,128)}), f32[160,10240]{1,0:T(8,128)}) %reduce-scatter.9.cloned.1.call-update) | async-done | bytes 6553616 | tf_op jit(solution)/shard_map/reduce_scatter | solution.py:211
  1984.6 18.2 fusion.15
  2021.1 12.6 fusion.116
  2033.6 22.6 reduce-scatter.15.cloned.1.call-done
  2066.4 13.2 fusion.54
  2079.6 42.7 %reduce-scatter.11.cloned.1.call-done = f32[12,160]{0,1:T(8,128)} async-done(((f32[12,1280]{0,1:T(8,128)}), f32[12,160]{0,1:T(8,128)}) %reduce-scatter.11.cloned.1.call-update) | async-done | bytes 7696 | tf_op jit(solution)/shard_map/reduce_scatter | solution.py:220
  2127.6 12.0 all-reduce
  2146.3 8.3 maximum_bitcast_fusion.2
  2154.6 35.4 %all-gather.10.cloned.1.call-done = f32[3,160,5120]{2,1,0:T(8,128)} async-done(((f32[3,160,1280]{2,1,0:T(8,128)}), f32[3,160,5120]{2,1,0:T(8,128)}) %all-gather.10.cloned.1.call-update) | async-done | bytes 9830416 | tf_op jit(solution)/shard_map/all_gather | solution.py:272
  2193.4 19.0 maximum_bitcast_fusion
  2218.6 97.3 %all-gather.12.cloned.1.call-done = f32[3,160,10240]{2,1,0:T(8,128)} async-done(((f32[3,160,2560]{2,1,0:T(8,128)}), f32[3,160,10240]{2,1,0:T(8,128)}) %all-gather.12.cloned.1.call-update) | async-done | bytes 19660816 | tf_op jit(solution)/shard_map/all_gather | solution.py:273
  2320.8 8.8 copy.180
  2329.6 15.0 copy.181
  (158 shorter events, 97.5 us)
Async XLA Ops:
  7.2 44.4 %copy-start = (s32[1,8]{1,0:T(1,128)S(1)}, s32[1,8]{1,0:T(1,128)}, u32[]{:S(2)}) copy-start(s32[1,8]{1,0:T(1,128)} %param.12) | copy-start | bytes 100
  7.2 189.3 %all-gather.6.cloned.1.call-start = ((), (), s32[]{:S(2)}) async-start(), calls=%async_computation.5 | async-start | bytes 14745600 | tf_op jit(solution)/shard_map/all_gather | solution.py:91
  10.6 686.3 %all-gather.8.cloned.1.call-start = ((), (), s32[]{:S(2)}) async-start(), calls=%async_computation.6 | async-start | bytes 29491200 | tf_op jit(solution)/shard_map/all_gather | solution.py:92
  15.6 38.6 %copy-start.5 = (bf16[128,1280]{1,0:T(8,128)(2,1)S(1)}, bf16[128,1280]{1,0:T(8,128)(2,1)}, u32[]{:S(2)}) copy-start(bf16[128,1280]{1,0:T(8,128)(2,1)} %param.10) | copy-start | bytes 983044
  15.6 1148.4 %reduce-scatter.7.cloned.1.call-start = ((), (), s32[]{:S(2)}) async-start(), calls=%async_computation.7 | async-start | bytes 29491200 | tf_op jit(solution)/shard_map/reduce_scatter | solution.py:203
  17.1 184.8 %copy-start.9 = (f32[1,12,160]{1,2,0:T(8,128)}, f32[1,12,160]{1,2,0:T(8,128)S(1)}, u32[]{:S(2)}) copy-start(f32[1,12,160]{1,2,0:T(8,128)S(1)} %copy.171) | copy-start | bytes 23044
  207.2 538.3 %copy-start.4 = (f32[128,1280]{1,0:T(8,128)}, f32[128,1280]{1,0:T(8,128)S(1)}, u32[]{:S(2)}) copy-start(f32[128,1280]{1,0:T(8,128)S(1)} %get-tuple-element.138) | copy-start | bytes 1966084
  702.8 11.3 copy-start.21
  714.1 8.4 copy-start.8
  745.5 13.2 copy-start.15
  745.5 1239.1 %reduce-scatter.9.cloned.1.call-start = ((), (), s32[]{:S(2)}) async-start(), calls=%async_computation.8 | async-start | bytes 58982400 | tf_op jit(solution)/shard_map/reduce_scatter | solution.py:211
  745.5 13.1 copy-start.22
  805.0 1212.5 %reduce-scatter.13.cloned.1.call-start = ((), (), s32[]{:S(2)}) async-start(), calls=%async_computation.10 | async-start | bytes 2048000 | tf_op jit(solution)/shard_map/reduce_scatter | solution.py:231
  1173.6 882.6 %reduce-scatter.15.cloned.1.call-start = ((), (), s32[]{:S(2)}) async-start(), calls=%async_computation.12 | async-start | bytes 4096000 | tf_op jit(solution)/shard_map/reduce_scatter | solution.py:237
  2002.9 119.4 %reduce-scatter.11.cloned.1.call-start = ((), (), s32[]{:S(2)}) async-start(), calls=%async_computation.9 | async-start | bytes 737280 | tf_op jit(solution)/shard_map/reduce_scatter | solution.py:220
  2017.5 172.6 %all-gather.10.cloned.1.call-start = ((), (), s32[]{:S(2)}) async-start(), calls=%async_computation.11 | async-start | bytes 12288000 | tf_op jit(solution)/shard_map/all_gather | solution.py:272
  2021.0 294.8 %all-gather.12.cloned.1.call-start = ((), (), s32[]{:S(2)}) async-start(), calls=%async_computation.13 | async-start | bytes 24576000 | tf_op jit(solution)/shard_map/all_gather | solution.py:273
  2066.4 55.9 %copy-start.10 = (f32[1,12,160]{1,2,0:T(8,128)S(1)}, f32[1,12,160]{1,2,0:T(8,128)}, u32[]{:S(2)}) copy-start(f32[1,12,160]{1,2,0:T(8,128)} %copy-done.9) | copy-start | bytes 23044
  2066.4 79.9 %copy-start.2 = (f32[160,5120]{1,0:T(8,128)S(1)}, f32[160,5120]{1,0:T(8,128)}, u32[]{:S(2)}) copy-start(f32[160,5120]{1,0:T(8,128)} %reduce-scatter.7.cloned.1.call-done) | copy-start | bytes 9830404
  2145.7 9.0 copy-start.16
  2193.3 19.0 slice-start
  2193.3 19.0 slice-start.1
  2193.3 19.7 copy-start.3
  2329.6 15.0 copy-start.1
  (10 other events, 31.1 us)
Sparse Core Ops, SparseCore 0:
  10.8 185.6 all-gather.5
  198.6 498.2 all-gather.7
  745.6 418.3 reduce-scatter.6
  1167.8 816.8 reduce-scatter.8
  1987.6 27.6 reduce-scatter.12
  2017.7 38.5 reduce-scatter.14
  2059.5 62.7 reduce-scatter.10
  2123.9 66.1 all-gather.9
  2191.6 124.1 all-gather.11
where the time goes:
time: 2360 us; the launch traced here: 2350 us
  waiting for transfers between devices  2000 us (85%)
  other arithmetic  119 us (5%)
  matrix products  91.1 us (4%)
  local copies, waits for them, and re-layouts  74.3 us (3%)
  blocking collectives  51.4 us (2%)
    reduce_scatter x1, waiting for transfers between devices, shards(): lax.psum_scatter(jnp.concatenate([contract_rows(layer_two, grad_pre), con...  811 us
    all_gather x1, waiting for transfers between devices, shards(): lax.all_gather(copies[1], 'fsdp', axis=0, tiled=True)  489 us
    reduce_scatter x1, waiting for transfers between devices, shards(): lax.psum_scatter(jnp.concatenate([contract_rows(layer_one, grad_qkv), con...  359 us
    all_gather x1, waiting for transfers between devices, shards(): lax.all_gather(copies[0], 'fsdp', axis=0, tiled=True)  142 us
    all_gather x1, waiting for transfers between devices, shards(): lax.all_gather(part_feedforward, 'rep', axis=2, tiled=True)  97.3 us
  transfers between devices with their start and end apart: 9, of which 8 were waited for; matrix products, arithmetic and copies ran while one was open for 9% of the time, Pallas kernels for 0%

commit v1 on v0

--- a/solution.py
+++ b/solution.py
@@ -17,6 +17,15 @@
 ADAM_EPS = 1e-08
 OUTER_RATE = 0.7
 OUTER_MOMENTUM = 0.5
+state_masks_now = lambda mine_x: jnp.concatenate(
+    lax.all_to_all(
+        jnp.stack([mine_x for _ in range(lax.axis_size("rep"))]),
+        axis_name="rep",
+        split_axis=0,
+        concat_axis=0,
+    ),
+    axis=2,
+)
 
 
 def contract_last(left, right):
@@ -270,7 +279,7 @@
     )
     next_attention, next_feedforward, next_vectors = (
         lax.all_gather(part_attention, "rep", axis=2, tiled=True),
-        lax.all_gather(part_feedforward, "rep", axis=2, tiled=True),
+        state_masks_now(part_feedforward),
         lax.all_gather(part_vectors, "rep", axis=1, tiled=True),
     )
     copy_attention = next_attention[2].astype(jnp.bfloat16)

time: 2360 us -> 2440 us (1.034)
  blocking collectives: 51.4 us -> 265 us
  waiting for transfers between devices: 2000 us -> 1850 us
    unnamed x1, blocking collectives: 12 us -> 226 us
    all_gather x1 -> x0, waiting for transfers between devices: 97.3 us -> none  [shards(): lax.all_gather(part_feedforward, 'rep', axis=2, tiled=True)]
    all_gather x1, waiting for transfers between devices: 35.4 us -> 0.01 us  [shards(): lax.all_gather(part_attention, 'rep', axis=2, tiled=True)]
  transfers between devices with their start and end apart: 9 -> 9, of which waited for: 8 -> 6; matrix products, arithmetic and copies ran while one was open for 9% -> 9% of each run, Pallas kernels for 0% -> 0%
where the time goes in v1:
time: 2440 us; the launch traced here: 2430 us
  waiting for transfers between devices  1850 us (76%)
  blocking collectives  265 us (11%)
  other arithmetic  117 us (5%)
  matrix products  89.5 us (4%)
  local copies, waits for them, and re-layouts  86.6 us (4%)
    reduce_scatter x1, waiting for transfers between devices, shards(): lax.psum_scatter(jnp.concatenate([contract_rows(layer_two, grad_pre), con...  811 us
    all_gather x1, waiting for transfers between devices, shards(): lax.all_gather(copies[1], 'fsdp', axis=0, tiled=True)  489 us
    reduce_scatter x1, waiting for transfers between devices, shards(): lax.psum_scatter(jnp.concatenate([contract_rows(layer_one, grad_qkv), con...  359 us
    unnamed x1, blocking collectives  226 us
    all_gather x1, waiting for transfers between devices, shards(): lax.all_gather(copies[0], 'fsdp', axis=0, tiled=True)  142 us
  transfers between devices with their start and end apart: 9, of which 6 were waited for; matrix products, arithmetic and copies ran while one was open for 9% of the time, Pallas kernels for 0%

profile of v1, /device:TPU:0, one launch (start us, length us, event | category | flops | bytes accessed | tf_op | source)
XLA Modules:
  0.0 2430.7 jit_solution(12266159200223745187)
XLA Ops:
  17.1 33.6 %all-gather = bf16[8,160,12]{1,2,0:T(8,128)(2,1)S(1)} all-gather(bf16[1,160,12]{1,2,0:T(8,128)(2,1)S(1)} %copy.146), channel_id=1, replica_groups=mesh['rep'=4,'fsdp'=8] {'fsdp'}, dimensions={0}, use_global_device_ids=true | all-gather | bytes 34560 | tf_op jit(solution)/shard_map/all_gather | solution.py:102
  54.6 141.9 %all-gather.5.cloned.1.call-done = bf16[1280,5120]{1,0:T(8,128)(2,1)} async-done(((bf16[160,5120]{1,0:T(8,128)(2,1)}), bf16[1280,5120]{1,0:T(8,128)(2,1)}) %all-gather.5.cloned.1.call-update) | async-done | bytes 13107216 | tf_op jit(solution)/shard_map/all_gather | solution.py:100
  207.5 489.4 %all-gather.7.cloned.1.call-done = bf16[1280,10240]{1,0:T(8,128)(2,1)} async-done(((bf16[160,10240]{1,0:T(8,128)(2,1)}), bf16[1280,10240]{1,0:T(8,128)(2,1)}) %all-gather.7.cloned.1.call-update) | async-done | bytes 26214416 | tf_op jit(solution)/shard_map/all_gather | solution.py:101
  702.8 11.3 convert_reduce_fusion
  714.1 8.1 multiply_reduce_fusion.1
  736.2 9.2 pad_maximum_fusion.1
  746.7 11.6 fusion.114
  758.3 12.3 fusion.109
  770.6 34.2 %pad_maximum_fusion = f32[1280,10240]{1,0:T(8,128)} fusion(f32[1280,5120]{1,0:T(8,128)} %fusion.109, f32[1280,5120]{1,0:T(8,128)} %fusion.114), kind=kLoop, calls=%fused_computation | loop fusion | flops 13107200 | bytes 104857600 | tf_op jit(solution)/shard_map/concatenate | solution.py:221
  804.9 359.0 %reduce-scatter.7.cloned.1.call-done = f32[160,5120]{1,0:T(8,128)} async-done(((f32[1280,5120]{1,0:T(8,128)}), f32[160,5120]{1,0:T(8,128)}) %reduce-scatter.7.cloned.1.call-update) | async-done | bytes 3276816 | tf_op jit(solution)/shard_map/reduce_scatter | solution.py:212
  1163.8 9.6 fusion.28
  1173.5 811.0 %reduce-scatter.9.cloned.1.call-done = f32[160,10240]{1,0:T(8,128)} async-done(((f32[1280,10240]{1,0:T(8,128)}), f32[160,10240]{1,0:T(8,128)}) %reduce-scatter.9.cloned.1.call-update) | async-done | bytes 6553616 | tf_op jit(solution)/shard_map/reduce_scatter | solution.py:220
  1984.5 18.2 fusion.15
  2003.2 6.5 fusion.116
  2021.0 12.6 fusion.115
  2033.6 22.5 reduce-scatter.15.cloned.1.call-done
  2061.5 12.0 stack.131
  2073.5 7.6 all-to-all-start
  2085.3 13.2 fusion.53
  2098.5 23.6 reduce-scatter.11.cloned.1.call-done
  2127.4 226.5 %all-reduce = bf16[12,160]{0,1:T(8,128)(2,1)S(1)} all-reduce(bf16[12,160]{0,1:T(8,128)(2,1)} %get-tuple-element.100), channel_id=7, replica_groups=mesh['rep'=4,'fsdp'=8] {'rep'}, use_global_device_ids=true, to_apply=%region_25.26.clone | all-reduce | flops 1920 | bytes 7680
  2360.2 8.3 maximum_bitcast_fusion.2
  2371.8 17.0 maximum_bitcast_fusion
  2394.4 17.1 copy.182
  (177 shorter events, 97.9 us)
Async XLA Ops:
  7.2 44.4 %copy-start = (s32[1,8]{1,0:T(1,128)S(1)}, s32[1,8]{1,0:T(1,128)}, u32[]{:S(2)}) copy-start(s32[1,8]{1,0:T(1,128)} %param.12) | copy-start | bytes 100
  7.2 189.3 %all-gather.5.cloned.1.call-start = ((), (), s32[]{:S(2)}) async-start(), calls=%async_computation.6 | async-start | bytes 14745600 | tf_op jit(solution)/shard_map/all_gather | solution.py:100
  10.6 686.3 %all-gather.7.cloned.1.call-start = ((), (), s32[]{:S(2)}) async-start(), calls=%async_computation.7 | async-start | bytes 29491200 | tf_op jit(solution)/shard_map/all_gather | solution.py:101
  15.6 38.6 %copy-start.7 = (bf16[128,1280]{1,0:T(8,128)(2,1)S(1)}, bf16[128,1280]{1,0:T(8,128)(2,1)}, u32[]{:S(2)}) copy-start(bf16[128,1280]{1,0:T(8,128)(2,1)} %param.10) | copy-start | bytes 983044
  15.6 1148.2 %reduce-scatter.7.cloned.1.call-start = ((), (), s32[]{:S(2)}) async-start(), calls=%async_computation.8 | async-start | bytes 29491200 | tf_op jit(solution)/shard_map/reduce_scatter | solution.py:212
  17.1 184.8 %copy-start.12 = (f32[1,12,160]{1,2,0:T(8,128)}, f32[1,12,160]{1,2,0:T(8,128)S(1)}, u32[]{:S(2)}) copy-start(f32[1,12,160]{1,2,0:T(8,128)S(1)} %copy.177) | copy-start | bytes 23044
  207.2 538.3 %copy-start.6 = (f32[128,1280]{1,0:T(8,128)}, f32[128,1280]{1,0:T(8,128)S(1)}, u32[]{:S(2)}) copy-start(f32[128,1280]{1,0:T(8,128)S(1)} %get-tuple-element.138) | copy-start | bytes 1966084
  702.8 11.3 copy-start.26
  745.4 12.9 copy-start.20
  745.4 1239.1 %reduce-scatter.9.cloned.1.call-start = ((), (), s32[]{:S(2)}) async-start(), calls=%async_computation.9 | async-start | bytes 58982400 | tf_op jit(solution)/shard_map/reduce_scatter | solution.py:220
  746.7 11.6 copy-start.27
  804.8 1212.8 %reduce-scatter.13.cloned.1.call-start = ((), (), s32[]{:S(2)}) async-start(), calls=%async_computation.11 | async-start | bytes 2048000 | tf_op jit(solution)/shard_map/reduce_scatter | solution.py:240
  1173.5 882.7 %reduce-scatter.15.cloned.1.call-start = ((), (), s32[]{:S(2)}) async-start(), calls=%async_computation.13 | async-start | bytes 4096000 | tf_op jit(solution)/shard_map/reduce_scatter | solution.py:246
  2002.8 119.3 %reduce-scatter.11.cloned.1.call-start = ((), (), s32[]{:S(2)}) async-start(), calls=%async_computation.10 | async-start | bytes 737280 | tf_op jit(solution)/shard_map/reduce_scatter | solution.py:229
  2017.5 351.0 %all-gather.9.cloned.1.call-start = ((), (), s32[]{:S(2)}) async-start(), calls=%async_computation.12 | async-start | bytes 12288000 | tf_op jit(solution)/shard_map/all_gather | solution.py:281
  2073.5 10.6 copy-start.5
  2073.5 320.8 %all-to-all-start = ((f32[4,3,160,2560]{3,2,1,0:T(8,128)}), f32[4,3,160,2560]{3,2,1,0:T(8,128)}, u32[]{:S(2)}, u32[]{:S(2)}) async-start(f32[4,3,160,2560]{3,2,1,0:T(8,128)} %stack.131), calls=%async_computation.5 | async-start | bytes 39321600 | tf_op jit(solution)/shard_map/all_to_all | solution.py:21
  2085.3 36.8 %copy-start.13 = (f32[1,12,160]{1,2,0:T(8,128)S(1)}, f32[1,12,160]{1,2,0:T(8,128)}, u32[]{:S(2)}) copy-start(f32[1,12,160]{1,2,0:T(8,128)} %copy-done.12) | copy-start | bytes 23044
  2085.3 274.9 %copy-start.2 = (f32[160,5120]{1,0:T(8,128)S(1)}, f32[160,5120]{1,0:T(8,128)}, u32[]{:S(2)}) copy-start(f32[160,5120]{1,0:T(8,128)} %reduce-scatter.7.cloned.1.call-done) | copy-start | bytes 9830404
  2371.8 17.0 slice-start
  2371.8 17.0 slice-start.1
  2371.8 17.0 copy-start.3
  2394.4 25.4 %slice-start.2 = ((s8[9830400]{0:T(1024)(128)(4,1)}), s8[4194304]{0:T(1024)(128)(4,1)S(1)}, s32[]{:S(2)}) async-start(s8[9830400]{0:T(1024)(128)(4,1)} %bitcast.217), calls=%async_computation.16 | async-start | bytes 8388608
  2394.4 25.4 %slice-start.3 = ((s8[9830400]{0:T(1024)(128)(4,1)}), s8[4194304]{0:T(1024)(128)(4,1)S(1)}, s32[]{:S(2)}) async-start(s8[9830400]{0:T(1024)(128)(4,1)} %bitcast.217), calls=%async_computation.17 | async-start | bytes 8388608
  (18 other events, 92.4 us)
Sparse Core Ops, SparseCore 0:
  10.8 185.6 all-gather.4
  198.6 498.2 all-gather.6
  745.5 418.2 reduce-scatter.6
  1167.6 816.8 reduce-scatter.8
  1987.5 27.6 reduce-scatter.12
  2017.6 38.5 reduce-scatter.14
  2059.4 62.6 reduce-scatter.10
  2123.7 118.3 all-gather.8
